TPU v7x, 32 devices: a whole 2x2x4 slice. The times are simulated.
32 devices in a mesh: hist: 16 (over z, x, core), orb: 2 (over y).
Axes of the slice: x: 2, y: 2, z: 4, core: 2. Of those that a mesh axis runs over, the one named last changes fastest.
Arguments:
- g_hist: bfloat16 [32, 64, 2048], P('hist', 'orb'), may hold values from -6 to 6
- sigma_hist: bfloat16 [2, 64, 2048], P(None, None, 'hist'), may hold values from -0.125 to 0.125
- diag_inv: float32 [32, 64, 64], P('hist'), may hold values from -0.75 to 0.75
- previous: float32 [2, 32, 64, 64], P(None, 'hist', 'orb'), may hold values from -6 to 6
- block_of_slot: int32 [16], replicated, may hold values from 0 to 15, each once
- front_pos: int32 [2], replicated, may hold values from 16 to 31
Outputs:
- g_row: float32 [2, 32, 64, 64], P(None, 'hist', 'orb')
- sigma_row: float32 [2, 32, 64, 64], P(None, 'hist', 'orb')
Inputs may be any that keep to these rules, and one draw needn't show every extreme that they name: `block_of_slot`: every block index appears once.
All inputs are finite; a program needn't handle non-finite values.
Results may differ from a plain program's by a relative error of at most 0.0003.
Values may be sent and summed in bfloat16 or wider, within the bound.
A program may use at most 64 MiB of HBM per device.

v0:
```python
import jax
import jax.numpy as jnp
from jax import lax
from jax.sharding import PartitionSpec as P

COUPLING = 0.5


def broadcast(value, axis, root):
    mine = lax.axis_index(axis) == root
    return lax.psum(jnp.where(mine, value, jnp.zeros_like(value)), axis)


def contract(g_piece, s_piece, times, col_time, front_pos):
    g_kept = jnp.where(
        (times[None, :] >= col_time[:, None])[:, None, :], g_piece, jnp.zeros_like(g_piece)
    )
    s_kept = jnp.where(
        (times[None, :] <= front_pos[:, None])[:, None, :], s_piece, jnp.zeros_like(s_piece)
    )
    return jnp.einsum("tcx,fax->ftca", g_kept, s_kept, preferred_element_type=jnp.float32)


def inverse_row(diag_inv, when, col_count):
    local = lax.dynamic_index_in_dim(diag_inv, when % col_count, 0, keepdims=False)
    return broadcast(local, "hist", when // col_count)


def body(g_hist, sigma_hist, diag_inv, previous, block_of_slot, front_pos):
    col_count = g_hist.shape[0]
    half_cols = g_hist.shape[1]
    orb_width = sigma_hist.shape[1]
    orb_id = lax.axis_index("orb")
    slot_id = lax.axis_index("hist")
    my_block = lax.dynamic_index_in_dim(block_of_slot, slot_id, 0, keepdims=False)
    col_time = my_block * col_count + jnp.arange(col_count, dtype=jnp.int32)
    piece = lax.all_gather(sigma_hist, "hist", axis=2, tiled=True)
    count = piece.shape[2]
    times = jnp.arange(count, dtype=jnp.int32) // orb_width
    integral = contract(g_hist, piece, times, col_time, front_pos)
    combined = previous + integral
    rows = jnp.stack([inverse_row(diag_inv, front_pos[front], col_count) for front in range(2)])
    g_row = jnp.einsum("ftcb,fab->ftca", combined, rows, precision=lax.Precision.HIGHEST)
    whole = lax.all_gather(g_row, "orb", axis=2, tiled=True)
    mirror = jnp.swapaxes(lax.dynamic_slice_in_dim(whole, orb_id * half_cols, half_cols, 3), 2, 3)
    sigma_row = COUPLING * g_row * g_row * mirror
    return (g_row, sigma_row)


def solution(mesh):
    in_specs = (
        P("hist", "orb", None),
        P(None, None, "hist"),
        P("hist", None, None),
        P(None, "hist", "orb", None),
        P(),
        P(),
    )
    out_specs = (P(None, "hist", "orb", None), P(None, "hist", "orb", None))
    return jax.shard_map(body, mesh=mesh, in_specs=in_specs, out_specs=out_specs, check_vma=False)
```

profile of v0, /device:TPU:0, one launch (start us, length us, event | category | flops | bytes accessed | tf_op | source)
XLA Modules:
  0.0 99.1 jit_solution(8734970899965628988)
XLA Ops:
  0.6 0.0 copy-start.4
  0.6 0.0 copy-start.3
  0.6 25.0 %all_gather.6 = bf16[2,64,2048]{2,1,0:T(8,128)(2,1)S(1)} all-gather(bf16[2,64,128]{2,1,0:T(8,128)(2,1)} %param.7), channel_id=1, replica_groups=mesh['hist'=16,'orb'=2] {'hist'}, dimensions={2}, use_global_device_ids=true | all-gather | bytes 557056 | tf_op jit(solution)/shard_map/all_gather | solution.py:37
  25.6 0.0 copy-start.5
  25.6 0.7 copy-done.5
  26.3 0.6 dynamic_slice.14
  27.5 0.0 copy-start.2
  27.5 0.6 copy-done.2
  28.2 0.1 broadcast_compare_fusion
  28.3 0.0 copy-done.4
  28.3 0.0 copy-done.3
  28.3 0.4 fusion
  28.7 0.0 copy-start.1
  28.7 0.6 fusion.18
  34.5 0.0 copy-done.1
  34.5 57.9 %all-reduce = (f32[1,64,64]{2,1,0:T(8,128)S(1)}, f32[1,64,64]{2,1,0:T(8,128)S(1)}) all-reduce(f32[1,64,64]{2,1,0:T(8,128)S(1)} %get-tuple-element.7, f32[1,64,64]{2,1,0:T(8,128)S(1)} %get-tuple-element.6), channel_id=1, replica_groups=mesh['hist'=16,'orb'=2] {'hist'}, use_global_device_ids=true, to_apply=%region_1.2 | all-reduce | flops 8192 | bytes 65536 | tf_op jit(solution)/shard_map/psum | solution.py:11
  92.4 0.2 fusion.10
  92.7 0.0 copy-start
  92.7 0.1 copy.8
  92.8 0.5 copy-done
  93.3 4.9 %all_gather.7 = f32[2,2,64,64]{3,2,1,0:T(8,128)S(1)} all-gather(f32[2,2,32,64]{3,2,1,0:T(8,128)S(1)} %fusion.10), channel_id=1, replica_groups=mesh['hist'=16,'orb'=2] {'orb'}, dimensions={2}, use_global_device_ids=true | all-gather | bytes 98304 | tf_op jit(solution)/shard_map/all_gather | solution.py:44
  98.2 0.1 fusion.8
  98.3 0.7 copy.10
  (3 shorter events, 0.0 us)
Async XLA Ops:
  0.6 27.6 %copy-start.4 = (f32[2,2,32,64]{3,2,1,0:T(8,128)S(1)}, f32[2,2,32,64]{3,2,1,0:T(8,128)}, u32[]{:S(2)}) copy-start(f32[2,2,32,64]{3,2,1,0:T(8,128)} %param.9) | copy-start | bytes 98308
  0.6 27.6 %copy-start.3 = (bf16[2,32,2048]{2,1,0:T(8,128)(2,1)S(1)}, bf16[2,32,2048]{2,1,0:T(8,128)(2,1)}, u32[]{:S(2)}) copy-start(bf16[2,32,2048]{2,1,0:T(8,128)(2,1)} %param.6) | copy-start | bytes 786436
  25.6 0.7 copy-start.5
  27.5 0.7 copy-start.2
  28.7 5.8 %copy-start.1 = (f32[2,64,64]{2,1,0:T(8,128)S(1)}, f32[2,64,64]{2,1,0:T(8,128)}, u32[]{:S(2)}) copy-start(f32[2,64,64]{2,1,0:T(8,128)} %param.8) | copy-start | bytes 98308
  92.7 0.6 copy-start
where the time goes:
time: 99.3 us; the launch traced here: 99.1 us
  blocking collectives  87.8 us (88%)
  between operations  6.62 us (7%)
  local copies, waits for them, and re-layouts  3.81 us (4%)
    psum x1, blocking collectives, broadcast(): return lax.psum(jnp.where(mine, value, jnp.zeros_like(value)), axis)  57.9 us
    all_gather x1, blocking collectives, body(): piece = lax.all_gather(sigma_hist, 'hist', axis=2, tiled=True)  25 us
    all_gather x1, blocking collectives, body(): whole = lax.all_gather(g_row, 'orb', axis=2, tiled=True)  4.92 us
    unnamed x13, local copies, waits for them, and re-layouts  2.55 us

commit v1 on v0

--- a/solution.py
+++ b/solution.py
@@ -8,7 +8,7 @@
 
 def broadcast(value, axis, root):
     mine = lax.axis_index(axis) == root
-    return lax.psum(jnp.where(mine, value, jnp.zeros_like(value)), axis)
+    return jnp.sum(lax.all_gather(jnp.where(mine, value, jnp.zeros_like(value)), axis), axis=0)
 
 
 def contract(g_piece, s_piece, times, col_time, front_pos):

time: 99.3 us -> 80.8 us (0.81)
  blocking collectives: 87.8 us -> 69.1 us
    psum x1 -> x0, blocking collectives: 57.9 us -> none  [broadcast(): return lax.psum(jnp.where(mine, value, jnp.zeros_like(value)), axis)]
    all_gather x0 -> x2, blocking collectives: none -> 39.2 us  [broadcast(): lax.all_gather(jnp.where(mine, value, jnp.zeros_like(value)), axis)]
where the time goes in v1:
time: 80.8 us; the launch traced here: 80.5 us
  blocking collectives  69.1 us (86%)
  between operations  6.63 us (8%)
  local copies, waits for them, and re-layouts  3.81 us (5%)
    all_gather x2, blocking collectives, broadcast(): lax.all_gather(jnp.where(mine, value, jnp.zeros_like(value)), axis)  39.2 us
    all_gather x1, blocking collectives, body(): piece = lax.all_gather(sigma_hist, 'hist', axis=2, tiled=True)  25 us
    all_gather x1, blocking collectives, body(): whole = lax.all_gather(g_row, 'orb', axis=2, tiled=True)  5 us
    unnamed x13, local copies, waits for them, and re-layouts  2.55 us

profile of v1, /device:TPU:0, one launch (start us, length us, event | category | flops | bytes accessed | tf_op | source)
XLA Modules:
  0.0 80.5 jit_solution(4416139007494817915)
XLA Ops:
  0.6 0.0 copy-start.4
  0.6 0.0 copy-start.3
  0.6 25.0 %all_gather.14 = bf16[2,64,2048]{2,1,0:T(8,128)(2,1)S(1)} all-gather(bf16[2,64,128]{2,1,0:T(8,128)(2,1)} %param.7), channel_id=1, replica_groups=mesh['hist'=16,'orb'=2] {'hist'}, dimensions={2}, use_global_device_ids=true | all-gather | bytes 557056 | tf_op jit(solution)/shard_map/all_gather | solution.py:37
  25.6 0.0 copy-start.5
  25.6 0.7 copy-done.5
  26.3 0.6 dynamic_slice.14
  27.5 0.0 copy-start.2
  27.5 0.6 copy-done.2
  28.2 0.1 broadcast_compare_fusion
  28.3 0.0 copy-done.4
  28.3 0.0 copy-done.3
  28.3 0.4 fusion
  28.7 0.0 copy-start.1
  28.7 0.6 fusion.18
  34.5 0.0 copy-done.1
  34.5 18.9 %all_gather.16 = f32[16,64,64]{2,1,0:T(8,128)S(1)} all-gather(f32[1,64,64]{2,1,0:T(8,128)S(1)} %get-tuple-element.7), channel_id=1, replica_groups=mesh['hist'=16,'orb'=2] {'hist'}, dimensions={0}, use_global_device_ids=true | all-gather | bytes 278528 | tf_op jit(solution)/shard_map/all_gather | solution.py:11
  53.4 20.3 %all_gather.15 = f32[16,64,64]{2,1,0:T(8,128)S(1)} all-gather(f32[1,64,64]{2,1,0:T(8,128)S(1)} %get-tuple-element.6), channel_id=1, replica_groups=mesh['hist'=16,'orb'=2] {'hist'}, dimensions={0}, use_global_device_ids=true | all-gather | bytes 278528 | tf_op jit(solution)/shard_map/all_gather | solution.py:11
  73.8 0.2 fusion.10
  74.0 0.0 copy-start
  74.0 0.1 copy.11
  74.1 0.5 copy-done
  74.7 5.0 %all_gather.17 = f32[2,2,64,64]{3,2,1,0:T(8,128)S(1)} all-gather(f32[2,2,32,64]{3,2,1,0:T(8,128)S(1)} %fusion.10), channel_id=1, replica_groups=mesh['hist'=16,'orb'=2] {'orb'}, dimensions={2}, use_global_device_ids=true | all-gather | bytes 98304 | tf_op jit(solution)/shard_map/all_gather | solution.py:44
  79.7 0.1 fusion.8
  79.8 0.7 copy.13
  (5 shorter events, 0.1 us)
Async XLA Ops:
  0.6 27.6 %copy-start.4 = (f32[2,2,32,64]{3,2,1,0:T(8,128)S(1)}, f32[2,2,32,64]{3,2,1,0:T(8,128)}, u32[]{:S(2)}) copy-start(f32[2,2,32,64]{3,2,1,0:T(8,128)} %param.9) | copy-start | bytes 98308
  0.6 27.6 %copy-start.3 = (bf16[2,32,2048]{2,1,0:T(8,128)(2,1)S(1)}, bf16[2,32,2048]{2,1,0:T(8,128)(2,1)}, u32[]{:S(2)}) copy-start(bf16[2,32,2048]{2,1,0:T(8,128)(2,1)} %param.6) | copy-start | bytes 786436
  25.6 0.7 copy-start.5
  27.5 0.7 copy-start.2
  28.7 5.8 %copy-start.1 = (f32[2,64,64]{2,1,0:T(8,128)S(1)}, f32[2,64,64]{2,1,0:T(8,128)}, u32[]{:S(2)}) copy-start(f32[2,64,64]{2,1,0:T(8,128)} %param.8) | copy-start | bytes 98308
  74.0 0.6 copy-start
